TPU v7x, 128 devices: a whole 4x4x4 slice. The times are simulated.
128 devices in a mesh: row: 16 (over y, x_hi, core), col: 8 (over x_lo, z).
Axes of the slice: x: 4 (x_hi: 2, x_lo: 2; x = x_hi * 2 + x_lo), y: 4, z: 4, core: 2. Of those that a mesh axis runs over, the one named last changes fastest.
Arguments:
- image: bfloat16 [768, 512, 256], P('row', 'col'), may hold values from -6 to 6
- norm_gain: float32 [2, 2, 256], replicated, may hold values from 0.1 to 1.9
- conv_first: bfloat16 [2, 3, 3, 256, 256], replicated, may hold values from -0.125 to 0.125
- conv_second: bfloat16 [2, 3, 3, 256, 256], replicated, may hold values from -0.125 to 0.125
- proj_in: bfloat16 [2, 256, 512], replicated, may hold values from -0.375 to 0.375
- block_mix: bfloat16 [2, 256, 256], replicated, may hold values from -0.375 to 0.375
- block_bias: float32 [2, 256], replicated, may hold values from 0.5 to 1.5
- grid_mix: bfloat16 [2, 128, 128], replicated, may hold values from -0.5 to 0.5
- grid_bias: float32 [2, 128], replicated, may hold values from 0.5 to 1.5
- proj_out: bfloat16 [2, 256, 256], replicated, may hold values from -0.375 to 0.375
Outputs:
- restored: bfloat16 [768, 512, 256], P('row', 'col')
All inputs are finite; a program needn't handle non-finite values.
Results may differ from a plain program's by a relative error of at most 0.012.
Values may be sent and summed in bfloat16 or wider, within the bound.
A program may use at most 128 MiB of HBM per device.

v0:
```python
import functools

import jax
import jax.numpy as jnp
from jax import lax
from jax.experimental import pallas as pl
from jax.experimental.pallas import tpu as pltpu
from jax.sharding import PartitionSpec as P

MESH = pl.DeviceIdType.MESH
F32 = jnp.float32
BF16 = jnp.bfloat16
LAYERS = 2
CH, CW, C, H = 48, 64, 256, 128
PIX = CH * CW
NROW, NCOL, CELLS = 16, 8, 128
SHARE = PIX // CELLS
OCT = SHARE // 8
EPS = 1e-06
GA = 0.7978845608028654
GB = GA * 0.044715


def gelu(v):
    h = 0.5 * v
    return h + h * jnp.tanh(v * (GA + GB * (v * v)))


def norm(v, gain):
    mean = jnp.sum(v, axis=-1, keepdims=True) * (1.0 / C)
    centred = v - mean
    var = jnp.sum(centred * centred, axis=-1, keepdims=True) * (1.0 / C)
    return centred * lax.rsqrt(var + EPS) * gain


def put_row(dst, u, y, left, right):
    at = pl.ds(pl.multiple_of(u * CW, CW), CW)
    j = lax.broadcasted_iota(jnp.int32, (CW, C), 0)
    dst[at, 0:C] = jnp.where(j == 0, left, pltpu.roll(y, 1, 0)).astype(BF16)
    dst[at, C : 2 * C] = y.astype(BF16)
    dst[at, 2 * C : 3 * C] = jnp.where(j == CW - 1, right, pltpu.roll(y, CW - 1, 0)).astype(BF16)


def kernel(
    image, gains, k1_hbm, k2_hbm, pin_hbm, bm_hbm, gm_hbm, pout_hbm, bbias, gbias,
    cur,
    k1, k2, pin, bmix, gmix, pout,
    X, F, MS, LU, LV, GU, GV, J, CBF, CB, HC, HV, HLF, RF, RECV, S32, MIX, GMV,
    w_sem, im_sem, hs_sem, hr_sem, as_sem, ar_sem, bs_sem, br_sem,
):
    row, col = lax.axis_index("row"), lax.axis_index("col")
    core = row % 2
    me = row * NCOL + col
    chip = (row // 2) * NCOL + col
    share = core * 64 + chip
    y0, xh, xl, z0 = row // 4, (row // 2) % 2, col // 4, col % 4

    def peer(k):
        k = (k * 37) % 64
        y = (y0 + k // 16) % 4
        h = (xh + (k // 8) % 2) % 2
        w = (xl + (k // 4) % 2) % 2
        z = (z0 + k % 4) % 4
        return y * 2 + h, w * 4 + z

    weights = ((k1_hbm, k1), (k2_hbm, k2), (pin_hbm, pin), (bm_hbm, bmix), (gm_hbm, gmix), (pout_hbm, pout))

    def weight(i, l):
        src, dst = weights[i]
        return pltpu.make_async_copy(src.at[l], dst.at[l], w_sem.at[l, i])

    load_image = pltpu.make_async_copy(image, cur, im_sem.at[0])
    load_image.start()
    for l in range(LAYERS):
        for i in range(len(weights)):
            weight(i, l).start()

    barrier = pltpu.get_barrier_semaphore()

    for kappa in range(2):

        def greet(k, carry):
            r2, c2 = peer(k)
            pl.semaphore_signal(barrier, inc=1, device_id=(r2 * 2 + kappa, c2), device_id_type=MESH)
            return carry

        lax.fori_loop((core == kappa).astype(jnp.int32), 64, greet, 0)

    load_image.wait()
    zero_row = jnp.zeros((1, C), F32)

    def layer(l, carry):
        gain0 = gains[pl.ds(2 * l, 1), :]
        gain1 = gains[pl.ds(2 * l + 1, 1), :]

        def norm_rows(c, carry):
            v = cur[pl.ds(pl.multiple_of(c * 256, 256), 256), :].astype(F32)
            n = norm(v, gain0)
            for r in range(4):
                y = n[r * CW : (r + 1) * CW]
                i = c * 4 + r
                put_row(X, i + 2, y, zero_row, zero_row)
                for slot, j in enumerate((0, 1, CW - 2, CW - 1)):
                    CBF[slot, pl.ds(i + 16, 1), :] = y[j : j + 1]
            return carry

        lax.fori_loop(0, CH // 4, norm_rows, 0)
        CB[...] = CBF[:, 16:64, :].astype(BF16)

        @pl.when(l == 0)
        def _():
            pl.semaphore_wait(barrier, CELLS - 1)

        up, down = (row + NROW - 1) % NROW, (row + 1) % NROW
        left, right = (col + NCOL - 1) % NCOL, (col + 1) % NCOL
        plan = (
            (X.at[2 * CW : 4 * CW, C : 2 * C], HV.at[l, 1], up, col),
            (X.at[CH * CW : (CH + 2) * CW, C : 2 * C], HV.at[l, 0], down, col),
            (CB.at[0:2], HC.at[l, 1, :, 16:64], row, left),
            (CB.at[2:4], HC.at[l, 0, :, 16:64], row, right),
            (CB.at[0:2, 0:16], HC.at[l, 1, :, 64:80], up, left),
            (CB.at[2:4, 0:16], HC.at[l, 0, :, 64:80], up, right),
            (CB.at[0:2, 32:48], HC.at[l, 1, :, 0:16], down, left),
            (CB.at[2:4, 32:48], HC.at[l, 0, :, 0:16], down, right),
        )
        halo = [
            pltpu.make_async_remote_copy(
                src_ref=src, dst_ref=dst, send_sem=hs_sem.at[l, i], recv_sem=hr_sem.at[l, i],
                device_id=(r, c), device_id_type=MESH,
            )
            for i, (src, dst, r, c) in enumerate(plan)
        ]
        for copy in halo:
            copy.start()
        weight(0, l).wait()
        for copy in halo:
            copy.wait()

        t80 = lax.broadcasted_iota(jnp.int32, (80, C), 0)
        outside = ((t80 < 16) & (row == 0)) | ((t80 >= 64) & (row == NROW - 1))
        for side, edge in ((0, col == 0), (1, col == NCOL - 1)):
            for k in range(2):
                HLF[side, k] = jnp.where(outside | edge, 0.0, HC[l, side, k].astype(F32))
        for u, part, edge in ((0, 0, row == 0), (1, 0, row == 0), (50, 1, row == NROW - 1), (51, 1, row == NROW - 1)):
            p = u % 2
            y = jnp.where(edge, 0.0, HV[l, part, p * CW : (p + 1) * CW, :].astype(F32))
            b = u + 14
            CBF[0, b : b + 1, :] = y[0:1]
            CBF[3, b : b + 1, :] = y[CW - 1 : CW]
            put_row(X, u, y, HLF[0, 1, b : b + 1, :], HLF[1, 0, b : b + 1, :])

        s16 = lax.broadcasted_iota(jnp.int32, (16, C), 0)

        def patch(i, carry):
            base = pl.multiple_of((i + 2) * CW, CW)
            a = X[pl.ds(base, 16), 0:C].astype(F32)
            X[pl.ds(base, 16), 0:C] = jnp.where(s16 == 0, HLF[0, 1, pl.ds(i + 16, 1), :], a).astype(BF16)
            b = X[pl.ds(base + CW - 16, 16), 2 * C :].astype(F32)
            X[pl.ds(base + CW - 16, 16), 2 * C :] = jnp.where(
                s16 == 15, HLF[1, 0, pl.ds(i + 16, 1), :], b
            ).astype(BF16)
            return carry

        lax.fori_loop(0, CH, patch, 0, unroll=4)

        acc = jnp.zeros((128, C), F32)
        for a in range(3):
            rows = slice(14 + a, 78 + a)
            lhs_left = jnp.concatenate([HLF[0, 0, rows, :], HLF[0, 1, rows, :], CBF[0, rows, :]], axis=1)
            lhs_right = jnp.concatenate([CBF[3, rows, :], HLF[1, 0, rows, :], HLF[1, 1, rows, :]], axis=1)
            lhs = jnp.concatenate([lhs_left, lhs_right], axis=0).astype(BF16)
            acc = acc + jnp.dot(lhs, k1[l, a * 768 : (a + 1) * 768, :], preferred_element_type=F32)
        rim = gelu(acc)
        t64 = lax.broadcasted_iota(jnp.int32, (64, C), 0)
        off = ((t64 == 0) & (row == 0)) | ((t64 == 49) & (row == NROW - 1))
        RF[0] = jnp.where(off | (col == 0), 0.0, rim[0:64])
        RF[1] = jnp.where(off | (col == NCOL - 1), 0.0, rim[64:128])

        def conv1(c, carry):
            base = c * 5
            lhs = jnp.concatenate(
                [X[pl.ds(pl.multiple_of((base + a) * CW, CW), 5 * CW), :] for a in range(3)], axis=1
            )
            y = gelu(jnp.dot(lhs, k1[l], preferred_element_type=F32))
            for r in range(5):
                t = base + r
                gone = ((t == 0) & (row == 0)) | ((t == CH + 1) & (row == NROW - 1))
                yr = jnp.where(gone, 0.0, y[r * CW : (r + 1) * CW])
                put_row(F, t, yr, RF[0, pl.ds(t, 1), :], RF[1, pl.ds(t, 1), :])
            return carry

        lax.fori_loop(0, 10, conv1, 0)
        weight(1, l).wait()
        weight(2, l).wait()

        def conv2(c, carry):
            at = pl.ds(pl.multiple_of(c * 256, 256), 256)
            lhs = jnp.concatenate(
                [F[pl.ds(pl.multiple_of((c * 4 + a) * CW, CW), 4 * CW), :] for a in range(3)], axis=1
            )
            m = cur[at, :].astype(F32) + jnp.dot(lhs, k2[l], preferred_element_type=F32)
            MS[at, :] = m
            n = norm(m, gain1).astype(BF16)
            e = gelu(jnp.dot(n, pin[l], preferred_element_type=F32))
            LU[at, :] = e[:, 0:H].astype(BF16)
            LV[at, :] = e[:, H : 2 * H].astype(BF16)
            GU[at, :] = e[:, 2 * H : 3 * H].astype(BF16)
            GV[l, pl.ds(pl.multiple_of(c * 32, 32), 32)] = e[:, 3 * H :].reshape(32, 8, H).astype(BF16)
            return carry

        def shares(c, kappa):
            return pl.ds(c * OCT, OCT)

        for kappa in range(2):
            lax.fori_loop(6 * kappa, 6 * kappa + 6, conv2, 0)

            def send(k, carry):
                r2, c2 = peer(k)
                d = kappa * 64 + r2 * NCOL + c2
                pltpu.make_async_remote_copy(
                    src_ref=GV.at[l, pl.ds(d * OCT, OCT)], dst_ref=RECV.at[l, pl.ds(me * OCT, OCT)],
                    send_sem=as_sem.at[l], recv_sem=ar_sem.at[l],
                    device_id=(r2 * 2 + kappa, c2), device_id_type=MESH,
                ).start()
                return carry

            lax.fori_loop((core == kappa).astype(jnp.int32), 64, send, 0)

        def mix():
            RECV[l, pl.ds(me * OCT, OCT)] = GV[l, pl.ds(share * OCT, OCT)]
            whole = RECV.at[l, pl.ds(0, (CELLS - 1) * OCT)]
            pltpu.make_async_copy(whole, whole, ar_sem.at[l]).wait()
            S32[...] = RECV[l].astype(F32).reshape(PIX, H)
            bias = jnp.broadcast_to(gbias[pl.ds(l, 1), :], (CELLS, CELLS)).T
            for q in range(0, SHARE, 4):
                rhs = jnp.concatenate(
                    [S32[pl.ds(q + i, CELLS, stride=SHARE), :].astype(BF16) for i in range(4)], axis=1
                )
                out = jnp.dot(gmix[l], rhs, preferred_element_type=F32)
                for i in range(4):
                    S32[pl.ds(q + i, CELLS, stride=SHARE), :] = out[:, i * H : (i + 1) * H] + bias
            MIX[l] = S32[...].reshape(CELLS * OCT, 8, H).astype(BF16)
            GMV[l, pl.ds(share * OCT, OCT)] = MIX[l, pl.ds(me * OCT, OCT)]
            for kappa in range(2):

                def back(k, carry):
                    r2, c2 = peer(k)
                    g = (r2 * 2 + kappa) * NCOL + c2
                    pltpu.make_async_remote_copy(
                        src_ref=MIX.at[l, pl.ds(g * OCT, OCT)], dst_ref=GMV.at[l, pl.ds(share * OCT, OCT)],
                        send_sem=bs_sem.at[l], recv_sem=br_sem.at[l, core],
                        device_id=(r2 * 2 + kappa, c2), device_id_type=MESH,
                    ).start()
                    return carry

                lax.fori_loop((core == kappa).astype(jnp.int32), 64, back, 0)

        weight(3, l).wait()
        weight(4, l).wait()
        weight(5, l).wait()
        pl.when(core == 0)(mix)

        lbias = jnp.broadcast_to(bbias[pl.ds(l, 1), :], (H, C)).T

        def block(s, carry):
            for half in range(2):
                cols = [slice((2 * half + i) * 16, (2 * half + i + 1) * 16) for i in range(2)]

                def rows(r, cs):
                    return pl.ds(pl.multiple_of((s * 16 + r) * CW + cs.start, 16), 16)

                rhs = jnp.concatenate(
                    [jnp.concatenate([LV[rows(r, cs), :] for r in range(16)], axis=0) for cs in cols], axis=1
                )
                lm = jnp.dot(bmix[l], rhs, preferred_element_type=F32)
                for i, cs in enumerate(cols):
                    for r in range(16):
                        part = lm[r * 16 : (r + 1) * 16, i * H : (i + 1) * H] + lbias[r * 16 : (r + 1) * 16]
                        J[rows(r, cs), 0:H] = (LU[rows(r, cs), :].astype(F32) * part).astype(BF16)
            return carry

        lax.fori_loop(0, CH // 16, block, 0)
        pl.when(core == 1)(mix)

        def finish(c, carry):
            at = pl.ds(pl.multiple_of(c * 256, 256), 256)
            gm = GMV[l, pl.ds(pl.multiple_of(c * 32, 32), 32)].astype(F32).reshape(256, H)
            gated = (GU[at, :].astype(F32) * gm).astype(BF16)
            joined = jnp.concatenate([J[at, 0:H], gated], axis=1)
            out = jnp.dot(joined, pout[l], preferred_element_type=F32)
            cur[at, :] = (MS[at, :] + out).astype(BF16)
            return carry

        for kappa in range(2):
            for own in range(2):

                @pl.when(core == own)
                def _():
                    some = GMV.at[l, pl.ds(0, (64 - (own == kappa)) * OCT)]
                    pltpu.make_async_copy(some, some, br_sem.at[l, kappa]).wait()

            lax.fori_loop(6 * kappa, 6 * kappa + 6, finish, 0)

        whole = GV.at[l, pl.ds(0, (CELLS - 1) * OCT)]
        pltpu.make_async_copy(whole, whole, as_sem.at[l]).wait()
        whole = MIX.at[l, pl.ds(0, (CELLS - 1) * OCT)]
        pltpu.make_async_copy(whole, whole, bs_sem.at[l]).wait()
        return carry

    lax.fori_loop(0, LAYERS, layer, 0)


def on_device(image, norm_gain, conv_first, conv_second, proj_in, block_mix, block_bias, grid_mix, grid_bias, proj_out):
    any_space = pl.BlockSpec(memory_space=pl.ANY)
    vmem = pl.BlockSpec(memory_space=pltpu.VMEM)
    V = pltpu.VMEM
    DMA = pltpu.SemaphoreType.DMA
    scratch = [
        V((LAYERS, 9 * C, C), BF16), V((LAYERS, 9 * C, C), BF16), V((LAYERS, C, 2 * C), BF16),
        V((LAYERS, C, C), BF16), V((LAYERS, CELLS, CELLS), BF16), V((LAYERS, C, C), BF16),
        V(((CH + 4) * CW, 3 * C), BF16), V(((CH + 2) * CW, 3 * C), BF16), V((PIX, C), F32),
        V((PIX, H), BF16), V((PIX, H), BF16), V((PIX, H), BF16), V((LAYERS, PIX // 8, 8, H), BF16), V((PIX, H), BF16),
        V((4, 80, C), F32), V((4, CH, C), BF16), V((LAYERS, 2, 2, 80, C), BF16), V((LAYERS, 2, 2 * CW, C), BF16),
        V((2, 2, 80, C), F32), V((2, 64, C), F32),
        V((LAYERS, PIX // 8, 8, H), BF16), V((PIX, H), F32), V((LAYERS, PIX // 8, 8, H), BF16),
        V((LAYERS, PIX // 8, 8, H), BF16),
        DMA((LAYERS, 6)), DMA((1,)), DMA((LAYERS, 8)), DMA((LAYERS, 8)),
        DMA((LAYERS,)), DMA((LAYERS,)), DMA((LAYERS,)), DMA((LAYERS, 2)),
    ]
    out = pl.pallas_call(
        kernel,
        out_shape=jax.ShapeDtypeStruct((PIX, C), BF16),
        in_specs=[any_space, vmem] + [any_space] * 6 + [vmem, vmem],
        out_specs=vmem,
        scratch_shapes=scratch,
        compiler_params=pltpu.CompilerParams(
            collective_id=0, has_side_effects=True, vmem_limit_bytes=62 * 2**20
        ),
    )(
        image.reshape(PIX, C), norm_gain.reshape(2 * LAYERS, C),
        conv_first.reshape(LAYERS, 9 * C, C), conv_second.reshape(LAYERS, 9 * C, C),
        proj_in, block_mix, grid_mix, proj_out, block_bias, grid_bias,
    )
    return out.reshape(image.shape)


def solution(mesh):
    placed = (P("row", "col", None), P(), P(), P(), P(), P(), P(), P(), P(), P())
    return jax.shard_map(
        on_device, mesh=mesh, in_specs=placed, out_specs=P("row", "col", None), check_vma=False
    )
```

profile of v0, /device:TPU:1, one launch (start us, length us, event | category | flops | bytes accessed | tf_op | source)
XLA Modules:
  0.0 119.2 jit_solution(10780725902746946595)
XLA Ops:
  0.0 1.3 %reshape.16.gains = f32[4,256]{1,0:T(4,128)} reshape(f32[2,2,256]{2,1,0:T(2,128)} %param.11) | data formatting | bytes 8192 | tf_op jit(solution)/shard_map/reshape | solution.py:340
  1.3 115.2 %shard_map.100 = bf16[3072,256]{1,0:T(8,128)(2,1)} custom-call(bf16[3072,256]{1,0:T(8,128)(2,1)} %bitcast.7, f32[4,256]{1,0:T(4,128)} %reshape.16.gains, bf16[2,2304,256]{2,1,0:T(8,128)(2,1)} %bitcast.5, bf16[2,2304,256]{2,1,0:T(8,128)(2,1)} %bitcast.6, bf16[2,256,512]{2,1,0:T(8,128)(2,1)} %pin_hbm.1, bf16[2,256,256]{2,1,0:T(8,128)(2,1)} %bm_hbm.1, ...), custom_call_target="tpu_custom_call" | custom-call | tf_op jit(solution)/shard_map/pallas_call | solution.py:330
  116.5 2.7 %copy.12 = bf16[48,64,256]{2,1,0:T(8,128)(2,1)} copy(bf16[48,64,256]{2,1,0:T(8,128)(2,1)} %bitcast.4) | data formatting | bytes 3145728
where the time goes:
time: 119 us
  Pallas kernels  115 us (97%)
  local copies, waits for them, and re-layouts  4.02 us (3%)
    pallas_call x1, Pallas kernels, on_device(): pl.pallas_call(kernel, out_shape=jax.ShapeDtypeStruct((PIX, C), BF16), in...  115 us
    unnamed x1, local copies, waits for them, and re-layouts  2.73 us

commit v1 on v0

--- a/solution.py
+++ b/solution.py
@@ -45,7 +45,7 @@
     image, gains, k1_hbm, k2_hbm, pin_hbm, bm_hbm, gm_hbm, pout_hbm, bbias, gbias,
     cur,
     k1, k2, pin, bmix, gmix, pout,
-    X, F, MS, LU, LV, GU, GV, J, CBF, CB, HC, HV, HLF, RF, RECV, S32, MIX, GMV,
+    X, F, MS, LU, LV, GU, GV, J, CBF, CB, HC, HV, HLF, RF, RECV, S32, MIX, GMV, A0, A1, B0, B1, E0, E1,
     w_sem, im_sem, hs_sem, hr_sem, as_sem, ar_sem, bs_sem, br_sem,
 ):
     row, col = lax.axis_index("row"), lax.axis_index("col")
@@ -63,6 +63,17 @@
         z = (z0 + k % 4) % 4
         return y * 2 + h, w * 4 + z
 
+    def to_group(kappa, act):
+        @pl.when(core != kappa)
+        def _():
+            act(0)
+
+        def step(k, carry):
+            act(k)
+            return carry
+
+        lax.fori_loop(1, 64, step, 0, unroll=7)
+
     weights = ((k1_hbm, k1), (k2_hbm, k2), (pin_hbm, pin), (bm_hbm, bmix), (gm_hbm, gmix), (pout_hbm, pout))
 
     def weight(i, l):
@@ -79,19 +90,18 @@
 
     for kappa in range(2):
 
-        def greet(k, carry):
+        def greet(k):
             r2, c2 = peer(k)
             pl.semaphore_signal(barrier, inc=1, device_id=(r2 * 2 + kappa, c2), device_id_type=MESH)
-            return carry
-
-        lax.fori_loop((core == kappa).astype(jnp.int32), 64, greet, 0)
+
+        to_group(kappa, greet)
 
     load_image.wait()
     zero_row = jnp.zeros((1, C), F32)
 
     def layer(l, carry):
-        gain0 = gains[pl.ds(2 * l, 1), :]
-        gain1 = gains[pl.ds(2 * l + 1, 1), :]
+        gain0 = gains[l, 0:1, :]
+        gain1 = gains[l, 1:2, :]
 
         def norm_rows(c, carry):
             v = cur[pl.ds(pl.multiple_of(c * 256, 256), 256), :].astype(F32)
@@ -104,7 +114,7 @@
                     CBF[slot, pl.ds(i + 16, 1), :] = y[j : j + 1]
             return carry
 
-        lax.fori_loop(0, CH // 4, norm_rows, 0)
+        lax.fori_loop(0, CH // 4, norm_rows, 0, unroll=2)
         CB[...] = CBF[:, 16:64, :].astype(BF16)
 
         @pl.when(l == 0)
@@ -176,45 +186,63 @@
         RF[0] = jnp.where(off | (col == 0), 0.0, rim[0:64])
         RF[1] = jnp.where(off | (col == NCOL - 1), 0.0, rim[64:128])
 
-        def conv1(c, carry):
+        def conv1_dot(c, acc):
             base = c * 5
             lhs = jnp.concatenate(
                 [X[pl.ds(pl.multiple_of((base + a) * CW, CW), 5 * CW), :] for a in range(3)], axis=1
             )
-            y = gelu(jnp.dot(lhs, k1[l], preferred_element_type=F32))
+            acc[...] = jnp.dot(lhs, k1[l], preferred_element_type=F32)
+
+        def conv1_rows(c, acc):
             for r in range(5):
-                t = base + r
+                t = c * 5 + r
                 gone = ((t == 0) & (row == 0)) | ((t == CH + 1) & (row == NROW - 1))
-                yr = jnp.where(gone, 0.0, y[r * CW : (r + 1) * CW])
-                put_row(F, t, yr, RF[0, pl.ds(t, 1), :], RF[1, pl.ds(t, 1), :])
-            return carry
-
-        lax.fori_loop(0, 10, conv1, 0)
-        weight(1, l).wait()
-        weight(2, l).wait()
-
-        def conv2(c, carry):
-            at = pl.ds(pl.multiple_of(c * 256, 256), 256)
+                y = jnp.where(gone, 0.0, gelu(acc[r * CW : (r + 1) * CW, :]))
+                put_row(F, t, y, RF[0, pl.ds(t, 1), :], RF[1, pl.ds(t, 1), :])
+
+        def conv1_pair(p, carry):
+            conv1_dot(2 * p + 1, A1)
+            conv1_rows(2 * p, A0)
+            conv1_dot(jnp.minimum(2 * p + 2, 9), A0)
+            conv1_rows(2 * p + 1, A1)
+            return carry
+
+        def conv2_dot(c, acc):
             lhs = jnp.concatenate(
                 [F[pl.ds(pl.multiple_of((c * 4 + a) * CW, CW), 4 * CW), :] for a in range(3)], axis=1
             )
-            m = cur[at, :].astype(F32) + jnp.dot(lhs, k2[l], preferred_element_type=F32)
+            acc[...] = jnp.dot(lhs, k2[l], preferred_element_type=F32)
+
+        def conv2_norm(c, acc, e):
+            at = pl.ds(pl.multiple_of(c * 256, 256), 256)
+            m = cur[at, :].astype(F32) + acc[...]
             MS[at, :] = m
             n = norm(m, gain1).astype(BF16)
-            e = gelu(jnp.dot(n, pin[l], preferred_element_type=F32))
-            LU[at, :] = e[:, 0:H].astype(BF16)
-            LV[at, :] = e[:, H : 2 * H].astype(BF16)
-            GU[at, :] = e[:, 2 * H : 3 * H].astype(BF16)
-            GV[l, pl.ds(pl.multiple_of(c * 32, 32), 32)] = e[:, 3 * H :].reshape(32, 8, H).astype(BF16)
-            return carry
-
-        def shares(c, kappa):
-            return pl.ds(c * OCT, OCT)
+            e[...] = jnp.dot(n, pin[l], preferred_element_type=F32)
+
+        def conv2_gelu(c, e):
+            at = pl.ds(pl.multiple_of(c * 256, 256), 256)
+            for h, dst in enumerate((LU, LV, GU)):
+                dst[at, :] = gelu(e[:, h * H : (h + 1) * H]).astype(BF16)
+            GV[l, pl.ds(pl.multiple_of(c * 32, 32), 32)] = gelu(e[:, 3 * H :]).reshape(32, 8, H).astype(BF16)
+
+        weight(1, l).wait()
+        weight(2, l).wait()
+        conv1_dot(0, A0)
 
         for kappa in range(2):
-            lax.fori_loop(6 * kappa, 6 * kappa + 6, conv2, 0)
-
-            def send(k, carry):
+            lax.fori_loop(3 * kappa, 3 + 2 * kappa, conv1_pair, 0)
+            accs, es = (B0, B1), (E0, E1)
+            first = 6 * kappa
+            for i in range(8):
+                if i < 6:
+                    conv2_dot(first + i, accs[i % 2])
+                if 1 <= i < 7:
+                    conv2_norm(first + i - 1, accs[(i - 1) % 2], es[(i - 1) % 2])
+                if i >= 2:
+                    conv2_gelu(first + i - 2, es[i % 2])
+
+            def send(k):
                 r2, c2 = peer(k)
                 d = kappa * 64 + r2 * NCOL + c2
                 pltpu.make_async_remote_copy(
@@ -222,9 +250,8 @@
                     send_sem=as_sem.at[l], recv_sem=ar_sem.at[l],
                     device_id=(r2 * 2 + kappa, c2), device_id_type=MESH,
                 ).start()
-                return carry
-
-            lax.fori_loop((core == kappa).astype(jnp.int32), 64, send, 0)
+
+            to_group(kappa, send)
 
         def mix():
             RECV[l, pl.ds(me * OCT, OCT)] = GV[l, pl.ds(share * OCT, OCT)]
@@ -243,7 +270,7 @@
             GMV[l, pl.ds(share * OCT, OCT)] = MIX[l, pl.ds(me * OCT, OCT)]
             for kappa in range(2):
 
-                def back(k, carry):
+                def back(k):
                     r2, c2 = peer(k)
                     g = (r2 * 2 + kappa) * NCOL + c2
                     pltpu.make_async_remote_copy(
@@ -251,9 +278,8 @@
                         send_sem=bs_sem.at[l], recv_sem=br_sem.at[l, core],
                         device_id=(r2 * 2 + kappa, c2), device_id_type=MESH,
                     ).start()
-                    return carry
-
-                lax.fori_loop((core == kappa).astype(jnp.int32), 64, back, 0)
+
+                to_group(kappa, back)
 
         weight(3, l).wait()
         weight(4, l).wait()
@@ -299,7 +325,7 @@
                     some = GMV.at[l, pl.ds(0, (64 - (own == kappa)) * OCT)]
                     pltpu.make_async_copy(some, some, br_sem.at[l, kappa]).wait()
 
-            lax.fori_loop(6 * kappa, 6 * kappa + 6, finish, 0)
+            lax.fori_loop(6 * kappa, 6 * kappa + 6, finish, 0, unroll=2)
 
         whole = GV.at[l, pl.ds(0, (CELLS - 1) * OCT)]
         pltpu.make_async_copy(whole, whole, as_sem.at[l]).wait()
@@ -324,6 +350,8 @@
         V((2, 2, 80, C), F32), V((2, 64, C), F32),
         V((LAYERS, PIX // 8, 8, H), BF16), V((PIX, H), F32), V((LAYERS, PIX // 8, 8, H), BF16),
         V((LAYERS, PIX // 8, 8, H), BF16),
+        V((5 * CW, C), F32), V((5 * CW, C), F32), V((4 * CW, C), F32), V((4 * CW, C), F32),
+        V((4 * CW, 2 * C), F32), V((4 * CW, 2 * C), F32),
         DMA((LAYERS, 6)), DMA((1,)), DMA((LAYERS, 8)), DMA((LAYERS, 8)),
         DMA((LAYERS,)), DMA((LAYERS,)), DMA((LAYERS,)), DMA((LAYERS, 2)),
     ]
@@ -337,7 +365,7 @@
             collective_id=0, has_side_effects=True, vmem_limit_bytes=62 * 2**20
         ),
     )(
-        image.reshape(PIX, C), norm_gain.reshape(2 * LAYERS, C),
+        image.reshape(PIX, C), norm_gain,
         conv_first.reshape(LAYERS, 9 * C, C), conv_second.reshape(LAYERS, 9 * C, C),
         proj_in, block_mix, grid_mix, proj_out, block_bias, grid_bias,
     )

time: 119 us -> 103 us (0.87)
  Pallas kernels: 115 us -> 100 us
  local copies, waits for them, and re-layouts: 4.02 us -> 2.73 us
    pallas_call x1, Pallas kernels: 115 us -> 100 us  [on_device(): pl.pallas_call(kernel, out_shape=jax.ShapeDtypeStruct((PIX, C), BF16), in...]
    reshape x1 -> x0, local copies, waits for them, and re-layouts: 1.29 us -> none  [on_device(): norm_gain.reshape(2 * LAYERS, C)]
where the time goes in v1:
time: 103 us
  Pallas kernels  100 us (97%)
  local copies, waits for them, and re-layouts  2.73 us (3%)
    pallas_call x1, Pallas kernels, on_device(): pl.pallas_call(kernel, out_shape=jax.ShapeDtypeStruct((PIX, C), BF16), in...  100 us
    unnamed x1, local copies, waits for them, and re-layouts  2.73 us

profile of v1, /device:TPU:1, one launch (start us, length us, event | category | flops | bytes accessed | tf_op | source)
XLA Modules:
  0.0 102.7 jit_solution(9028056985012339348)
XLA Ops:
  0.0 100.0 %shard_map.100 = bf16[3072,256]{1,0:T(8,128)(2,1)} custom-call(bf16[3072,256]{1,0:T(8,128)(2,1)} %bitcast.7, f32[2,2,256]{2,1,0:T(2,128)} %gains.1, bf16[2,2304,256]{2,1,0:T(8,128)(2,1)} %bitcast.5, bf16[2,2304,256]{2,1,0:T(8,128)(2,1)} %bitcast.6, bf16[2,256,512]{2,1,0:T(8,128)(2,1)} %pin_hbm.1, bf16[2,256,256]{2,1,0:T(8,128)(2,1)} %bm_hbm.1, ...), custom_call_target="tpu_custom_call" | custom-call | tf_op jit(solution)/shard_map/pallas_call | solution.py:358
  100.0 2.7 %copy.12 = bf16[48,64,256]{2,1,0:T(8,128)(2,1)} copy(bf16[48,64,256]{2,1,0:T(8,128)(2,1)} %bitcast.4) | data formatting | bytes 3145728

commit v2 on v1

--- a/solution.py
+++ b/solution.py
@@ -99,22 +99,24 @@
     load_image.wait()
     zero_row = jnp.zeros((1, C), F32)
 
+    def norm_rows(c, v, gain):
+        n = norm(v, gain)
+        for r in range(4):
+            y = n[r * CW : (r + 1) * CW]
+            i = c * 4 + r
+            put_row(X, i + 2, y, zero_row, zero_row)
+            for slot, j in enumerate((0, 1, CW - 2, CW - 1)):
+                CBF[slot, pl.ds(i + 16, 1), :] = y[j : j + 1]
+
+    def first_norm(c, carry):
+        v = cur[pl.ds(pl.multiple_of(c * 256, 256), 256), :].astype(F32)
+        norm_rows(c, v, gains[0, 0:1, :])
+        return carry
+
+    lax.fori_loop(0, CH // 4, first_norm, 0, unroll=2)
+
     def layer(l, carry):
-        gain0 = gains[l, 0:1, :]
         gain1 = gains[l, 1:2, :]
-
-        def norm_rows(c, carry):
-            v = cur[pl.ds(pl.multiple_of(c * 256, 256), 256), :].astype(F32)
-            n = norm(v, gain0)
-            for r in range(4):
-                y = n[r * CW : (r + 1) * CW]
-                i = c * 4 + r
-                put_row(X, i + 2, y, zero_row, zero_row)
-                for slot, j in enumerate((0, 1, CW - 2, CW - 1)):
-                    CBF[slot, pl.ds(i + 16, 1), :] = y[j : j + 1]
-            return carry
-
-        lax.fori_loop(0, CH // 4, norm_rows, 0, unroll=2)
         CB[...] = CBF[:, 16:64, :].astype(BF16)
 
         @pl.when(l == 0)
@@ -142,7 +144,53 @@
         ]
         for copy in halo:
             copy.start()
+        def conv1_dot(c, acc):
+            base = c * 5
+            lhs = jnp.concatenate(
+                [X[pl.ds(pl.multiple_of((base + a) * CW, CW), 5 * CW), :] for a in range(3)], axis=1
+            )
+            acc[...] = jnp.dot(lhs, k1[l], preferred_element_type=F32)
+
+        def conv1_rows(c, acc, edges):
+            for r in range(5):
+                t = c * 5 + r
+                y = gelu(acc[r * CW : (r + 1) * CW, :])
+                if t in (0, CH + 1):
+                    y = jnp.where((row == 0) if t == 0 else (row == NROW - 1), 0.0, y)
+                if edges:
+                    y = jnp.where(j64 == 0, RF[1, t : t + 1, :], jnp.where(j64 == CW - 1, RF[2, t : t + 1, :], y))
+                    put_row(F, t, y, RF[0, t : t + 1, :], RF[3, t : t + 1, :])
+                else:
+                    put_row(F, t, y, zero_row, zero_row)
+
+        def conv1(chunks, edges):
+            conv1_dot(chunks[0], A0)
+            for i, c in enumerate(chunks):
+                if c + 1 in chunks:
+                    conv1_dot(c + 1, (A1, A0)[i % 2])
+                conv1_rows(c, (A0, A1)[i % 2], edges)
+
+        def patch(t, carry):
+            base = pl.multiple_of(t * CW, CW)
+            edge = [RF[k, pl.ds(t, 1), :] for k in range(4)]
+            lo, hi = pl.ds(base, 16), pl.ds(base + CW - 16, 16)
+            for at, lanes, fixes in (
+                (lo, slice(0, C), ((0, 0), (1, 1))),
+                (lo, slice(C, 2 * C), ((0, 1),)),
+                (hi, slice(C, 2 * C), ((15, 2),)),
+                (hi, slice(2 * C, 3 * C), ((14, 2), (15, 3))),
+            ):
+                v = F[at, lanes].astype(F32)
+                for place, k in fixes:
+                    v = jnp.where(s16 == place, edge[k], v)
+                F[at, lanes] = v.astype(BF16)
+            return carry
+
+        s16 = lax.broadcasted_iota(jnp.int32, (16, C), 0)
+        j64 = lax.broadcasted_iota(jnp.int32, (CW, C), 0)
         weight(0, l).wait()
+
+        conv1(range(1, 6), False)
         for copy in halo:
             copy.wait()
 
@@ -155,57 +203,22 @@
             p = u % 2
             y = jnp.where(edge, 0.0, HV[l, part, p * CW : (p + 1) * CW, :].astype(F32))
             b = u + 14
-            CBF[0, b : b + 1, :] = y[0:1]
-            CBF[3, b : b + 1, :] = y[CW - 1 : CW]
-            put_row(X, u, y, HLF[0, 1, b : b + 1, :], HLF[1, 0, b : b + 1, :])
-
-        s16 = lax.broadcasted_iota(jnp.int32, (16, C), 0)
-
-        def patch(i, carry):
-            base = pl.multiple_of((i + 2) * CW, CW)
-            a = X[pl.ds(base, 16), 0:C].astype(F32)
-            X[pl.ds(base, 16), 0:C] = jnp.where(s16 == 0, HLF[0, 1, pl.ds(i + 16, 1), :], a).astype(BF16)
-            b = X[pl.ds(base + CW - 16, 16), 2 * C :].astype(F32)
-            X[pl.ds(base + CW - 16, 16), 2 * C :] = jnp.where(
-                s16 == 15, HLF[1, 0, pl.ds(i + 16, 1), :], b
-            ).astype(BF16)
-            return carry
-
-        lax.fori_loop(0, CH, patch, 0, unroll=4)
-
-        acc = jnp.zeros((128, C), F32)
+            for slot, j in enumerate((0, 1, CW - 2, CW - 1)):
+                CBF[slot, b : b + 1, :] = y[j : j + 1]
+            put_row(X, u, y, zero_row, zero_row)
+
+        columns = [HLF.at[0, 0], HLF.at[0, 1]] + [CBF.at[k] for k in range(4)] + [HLF.at[1, 0], HLF.at[1, 1]]
+        acc = jnp.zeros((256, C), F32)
         for a in range(3):
-            rows = slice(14 + a, 78 + a)
-            lhs_left = jnp.concatenate([HLF[0, 0, rows, :], HLF[0, 1, rows, :], CBF[0, rows, :]], axis=1)
-            lhs_right = jnp.concatenate([CBF[3, rows, :], HLF[1, 0, rows, :], HLF[1, 1, rows, :]], axis=1)
-            lhs = jnp.concatenate([lhs_left, lhs_right], axis=0).astype(BF16)
+            part = [ref[14 + a : 78 + a, :].astype(BF16) for ref in columns]
+            lhs = jnp.concatenate(
+                [jnp.concatenate(part[k : k + 3], axis=1) for k in (0, 1, 4, 5)], axis=0
+            )
             acc = acc + jnp.dot(lhs, k1[l, a * 768 : (a + 1) * 768, :], preferred_element_type=F32)
         rim = gelu(acc)
-        t64 = lax.broadcasted_iota(jnp.int32, (64, C), 0)
-        off = ((t64 == 0) & (row == 0)) | ((t64 == 49) & (row == NROW - 1))
-        RF[0] = jnp.where(off | (col == 0), 0.0, rim[0:64])
-        RF[1] = jnp.where(off | (col == NCOL - 1), 0.0, rim[64:128])
-
-        def conv1_dot(c, acc):
-            base = c * 5
-            lhs = jnp.concatenate(
-                [X[pl.ds(pl.multiple_of((base + a) * CW, CW), 5 * CW), :] for a in range(3)], axis=1
-            )
-            acc[...] = jnp.dot(lhs, k1[l], preferred_element_type=F32)
-
-        def conv1_rows(c, acc):
-            for r in range(5):
-                t = c * 5 + r
-                gone = ((t == 0) & (row == 0)) | ((t == CH + 1) & (row == NROW - 1))
-                y = jnp.where(gone, 0.0, gelu(acc[r * CW : (r + 1) * CW, :]))
-                put_row(F, t, y, RF[0, pl.ds(t, 1), :], RF[1, pl.ds(t, 1), :])
-
-        def conv1_pair(p, carry):
-            conv1_dot(2 * p + 1, A1)
-            conv1_rows(2 * p, A0)
-            conv1_dot(jnp.minimum(2 * p + 2, 9), A0)
-            conv1_rows(2 * p + 1, A1)
-            return carry
+        off = ((j64 == 0) & (row == 0)) | ((j64 == CH + 1) & (row == NROW - 1))
+        for k, edge in enumerate((col == 0, False, False, col == NCOL - 1)):
+            RF[k] = jnp.where(off | edge, 0.0, rim[k * 64 : (k + 1) * 64])
 
         def conv2_dot(c, acc):
             lhs = jnp.concatenate(
@@ -228,10 +241,12 @@
 
         weight(1, l).wait()
         weight(2, l).wait()
-        conv1_dot(0, A0)
-
         for kappa in range(2):
-            lax.fori_loop(3 * kappa, 3 + 2 * kappa, conv1_pair, 0)
+            if kappa == 0:
+                conv1(range(0, 1), True)
+                lax.fori_loop(5, 30, patch, 0, unroll=5)
+            else:
+                conv1(range(6, 10), True)
             accs, es = (B0, B1), (E0, E1)
             first = 6 * kappa
             for i in range(8):
@@ -308,13 +323,22 @@
         lax.fori_loop(0, CH // 16, block, 0)
         pl.when(core == 1)(mix)
 
-        def finish(c, carry):
+        def finish(c):
             at = pl.ds(pl.multiple_of(c * 256, 256), 256)
             gm = GMV[l, pl.ds(pl.multiple_of(c * 32, 32), 32)].astype(F32).reshape(256, H)
             gated = (GU[at, :].astype(F32) * gm).astype(BF16)
             joined = jnp.concatenate([J[at, 0:H], gated], axis=1)
             out = jnp.dot(joined, pout[l], preferred_element_type=F32)
-            cur[at, :] = (MS[at, :] + out).astype(BF16)
+            done = (MS[at, :] + out).astype(BF16)
+            cur[at, :] = done
+            return done
+
+        def middle(c, carry):
+            norm_rows(c, finish(c).astype(F32), gains[jnp.minimum(l + 1, LAYERS - 1), 0:1, :])
+            return carry
+
+        def last(c, carry):
+            finish(c)
             return carry
 
         for kappa in range(2):
@@ -325,7 +349,13 @@
                     some = GMV.at[l, pl.ds(0, (64 - (own == kappa)) * OCT)]
                     pltpu.make_async_copy(some, some, br_sem.at[l, kappa]).wait()
 
-            lax.fori_loop(6 * kappa, 6 * kappa + 6, finish, 0, unroll=2)
+            @pl.when(l < LAYERS - 1)
+            def _():
+                lax.fori_loop(6 * kappa, 6 * kappa + 6, middle, 0, unroll=2)
+
+            @pl.when(l == LAYERS - 1)
+            def _():
+                lax.fori_loop(6 * kappa, 6 * kappa + 6, last, 0, unroll=2)
 
         whole = GV.at[l, pl.ds(0, (CELLS - 1) * OCT)]
         pltpu.make_async_copy(whole, whole, as_sem.at[l]).wait()
@@ -347,7 +377,7 @@
         V(((CH + 4) * CW, 3 * C), BF16), V(((CH + 2) * CW, 3 * C), BF16), V((PIX, C), F32),
         V((PIX, H), BF16), V((PIX, H), BF16), V((PIX, H), BF16), V((LAYERS, PIX // 8, 8, H), BF16), V((PIX, H), BF16),
         V((4, 80, C), F32), V((4, CH, C), BF16), V((LAYERS, 2, 2, 80, C), BF16), V((LAYERS, 2, 2 * CW, C), BF16),
-        V((2, 2, 80, C), F32), V((2, 64, C), F32),
+        V((2, 2, 80, C), F32), V((4, 64, C), F32),
         V((LAYERS, PIX // 8, 8, H), BF16), V((PIX, H), F32), V((LAYERS, PIX // 8, 8, H), BF16),
         V((LAYERS, PIX // 8, 8, H), BF16),
         V((5 * CW, C), F32), V((5 * CW, C), F32), V((4 * CW, C), F32), V((4 * CW, C), F32),

time: 103 us -> 94.9 us (0.921)
  Pallas kernels: 100 us -> 92 us
    pallas_call x1, Pallas kernels: 100 us -> 92 us  [on_device(): pl.pallas_call(kernel, out_shape=jax.ShapeDtypeStruct((PIX, C), BF16), in...]
where the time goes in v2:
time: 94.9 us; the launch traced here: 94.8 us
  Pallas kernels  92 us (97%)
  local copies, waits for them, and re-layouts  2.73 us (3%)
    pallas_call x1, Pallas kernels, on_device(): pl.pallas_call(kernel, out_shape=jax.ShapeDtypeStruct((PIX, C), BF16), in...  92 us
    unnamed x1, local copies, waits for them, and re-layouts  2.73 us

profile of v2, /device:TPU:1, one launch (start us, length us, event | category | flops | bytes accessed | tf_op | source)
XLA Modules:
  0.0 94.8 jit_solution(16657881425477935744)
XLA Ops:
  0.0 92.0 %shard_map.100 = bf16[3072,256]{1,0:T(8,128)(2,1)} custom-call(bf16[3072,256]{1,0:T(8,128)(2,1)} %bitcast.7, f32[2,2,256]{2,1,0:T(2,128)} %gains.1, bf16[2,2304,256]{2,1,0:T(8,128)(2,1)} %bitcast.5, bf16[2,2304,256]{2,1,0:T(8,128)(2,1)} %bitcast.6, bf16[2,256,512]{2,1,0:T(8,128)(2,1)} %pin_hbm.1, bf16[2,256,256]{2,1,0:T(8,128)(2,1)} %bm_hbm.1, ...), custom_call_target="tpu_custom_call" | custom-call | tf_op jit(solution)/shard_map/pallas_call | solution.py:388
  92.0 2.7 %copy.12 = bf16[48,64,256]{2,1,0:T(8,128)(2,1)} copy(bf16[48,64,256]{2,1,0:T(8,128)(2,1)} %bitcast.4) | data formatting | bytes 3145728

commit v3 on v2

--- a/solution.py
+++ b/solution.py
@@ -42,37 +42,32 @@
 
 
 def kernel(
-    image, gains, k1_hbm, k2_hbm, pin_hbm, bm_hbm, gm_hbm, pout_hbm, bbias, gbias,
-    cur,
+    image, gains_hbm, k1_hbm, k2_hbm, pin_hbm, bm_hbm, gm_hbm, pout_hbm, bbias_hbm, gbias_hbm,
+    result,
+    cur, gains, bbias, gbias,
     k1, k2, pin, bmix, gmix, pout,
     X, F, MS, LU, LV, GU, GV, J, CBF, CB, HC, HV, HLF, RF, RECV, S32, MIX, GMV, A0, A1, B0, B1, E0, E1,
-    w_sem, im_sem, hs_sem, hr_sem, as_sem, ar_sem, bs_sem, br_sem,
+    w_sem, im_sem, out_sem, hs_sem, hr_sem, as_sem, ar_sem, bs_sem, br_sem,
 ):
     row, col = lax.axis_index("row"), lax.axis_index("col")
     core = row % 2
     me = row * NCOL + col
     chip = (row // 2) * NCOL + col
     share = core * 64 + chip
-    y0, xh, xl, z0 = row // 4, (row // 2) % 2, col // 4, col % 4
-
-    def peer(k):
-        k = (k * 37) % 64
-        y = (y0 + k // 16) % 4
-        h = (xh + (k // 8) % 2) % 2
-        w = (xl + (k // 4) % 2) % 2
-        z = (z0 + k % 4) % 4
-        return y * 2 + h, w * 4 + z
+    half_row = lax.div(row, 2)
+    columns_from = [lax.rem(col + j, NCOL) for j in range(NCOL)]
 
     def to_group(kappa, act):
-        @pl.when(core != kappa)
-        def _():
-            act(0)
-
-        def step(k, carry):
-            act(k)
+        def step(o, carry):
+            for j in range(NCOL):
+                r2 = lax.rem(half_row + o + j, 8)
+                if j == 0:
+                    pl.when((o != 0) | (core != kappa))(functools.partial(act, r2, columns_from[j]))
+                else:
+                    act(r2, columns_from[j])
             return carry
 
-        lax.fori_loop(1, 64, step, 0, unroll=7)
+        lax.fori_loop(0, 8, step, 0)
 
     weights = ((k1_hbm, k1), (k2_hbm, k2), (pin_hbm, pin), (bm_hbm, bmix), (gm_hbm, gmix), (pout_hbm, pout))
 
@@ -82,6 +77,12 @@
 
     load_image = pltpu.make_async_copy(image, cur, im_sem.at[0])
     load_image.start()
+    small = [
+        pltpu.make_async_copy(src, dst, im_sem.at[1 + i])
+        for i, (src, dst) in enumerate(((gains_hbm, gains), (bbias_hbm, bbias), (gbias_hbm, gbias)))
+    ]
+    for copy in small:
+        copy.start()
     for l in range(LAYERS):
         for i in range(len(weights)):
             weight(i, l).start()
@@ -90,13 +91,14 @@
 
     for kappa in range(2):
 
-        def greet(k):
-            r2, c2 = peer(k)
+        def greet(r2, c2):
             pl.semaphore_signal(barrier, inc=1, device_id=(r2 * 2 + kappa, c2), device_id_type=MESH)
 
         to_group(kappa, greet)
 
     load_image.wait()
+    for copy in small:
+        copy.wait()
     zero_row = jnp.zeros((1, C), F32)
 
     def norm_rows(c, v, gain):
@@ -257,8 +259,7 @@
                 if i >= 2:
                     conv2_gelu(first + i - 2, es[i % 2])
 
-            def send(k):
-                r2, c2 = peer(k)
+            def send(r2, c2):
                 d = kappa * 64 + r2 * NCOL + c2
                 pltpu.make_async_remote_copy(
                     src_ref=GV.at[l, pl.ds(d * OCT, OCT)], dst_ref=RECV.at[l, pl.ds(me * OCT, OCT)],
@@ -285,8 +286,7 @@
             GMV[l, pl.ds(share * OCT, OCT)] = MIX[l, pl.ds(me * OCT, OCT)]
             for kappa in range(2):
 
-                def back(k):
-                    r2, c2 = peer(k)
+                def back(r2, c2):
                     g = (r2 * 2 + kappa) * NCOL + c2
                     pltpu.make_async_remote_copy(
                         src_ref=MIX.at[l, pl.ds(g * OCT, OCT)], dst_ref=GMV.at[l, pl.ds(share * OCT, OCT)],
@@ -356,6 +356,7 @@
             @pl.when(l == LAYERS - 1)
             def _():
                 lax.fori_loop(6 * kappa, 6 * kappa + 6, last, 0, unroll=2)
+                store(kappa).start()
 
         whole = GV.at[l, pl.ds(0, (CELLS - 1) * OCT)]
         pltpu.make_async_copy(whole, whole, as_sem.at[l]).wait()
@@ -363,15 +364,21 @@
         pltpu.make_async_copy(whole, whole, bs_sem.at[l]).wait()
         return carry
 
+    def store(kappa):
+        half = pl.ds(kappa * (PIX // 2), PIX // 2)
+        return pltpu.make_async_copy(cur.at[half], result.at[half], out_sem.at[kappa])
+
     lax.fori_loop(0, LAYERS, layer, 0)
+    for kappa in range(2):
+        store(kappa).wait()
 
 
 def on_device(image, norm_gain, conv_first, conv_second, proj_in, block_mix, block_bias, grid_mix, grid_bias, proj_out):
     any_space = pl.BlockSpec(memory_space=pl.ANY)
-    vmem = pl.BlockSpec(memory_space=pltpu.VMEM)
     V = pltpu.VMEM
     DMA = pltpu.SemaphoreType.DMA
     scratch = [
+        V((PIX, C), BF16), V((LAYERS, 2, C), F32), V((LAYERS, C), F32), V((LAYERS, CELLS), F32),
         V((LAYERS, 9 * C, C), BF16), V((LAYERS, 9 * C, C), BF16), V((LAYERS, C, 2 * C), BF16),
         V((LAYERS, C, C), BF16), V((LAYERS, CELLS, CELLS), BF16), V((LAYERS, C, C), BF16),
         V(((CH + 4) * CW, 3 * C), BF16), V(((CH + 2) * CW, 3 * C), BF16), V((PIX, C), F32),
@@ -382,14 +389,14 @@
         V((LAYERS, PIX // 8, 8, H), BF16),
         V((5 * CW, C), F32), V((5 * CW, C), F32), V((4 * CW, C), F32), V((4 * CW, C), F32),
         V((4 * CW, 2 * C), F32), V((4 * CW, 2 * C), F32),
-        DMA((LAYERS, 6)), DMA((1,)), DMA((LAYERS, 8)), DMA((LAYERS, 8)),
+        DMA((LAYERS, 6)), DMA((4,)), DMA((2,)), DMA((LAYERS, 8)), DMA((LAYERS, 8)),
         DMA((LAYERS,)), DMA((LAYERS,)), DMA((LAYERS,)), DMA((LAYERS, 2)),
     ]
     out = pl.pallas_call(
         kernel,
         out_shape=jax.ShapeDtypeStruct((PIX, C), BF16),
-        in_specs=[any_space, vmem] + [any_space] * 6 + [vmem, vmem],
-        out_specs=vmem,
+        in_specs=[any_space] * 10,
+        out_specs=any_space,
         scratch_shapes=scratch,
         compiler_params=pltpu.CompilerParams(
             collective_id=0, has_side_effects=True, vmem_limit_bytes=62 * 2**20

time: 94.9 us -> 88.9 us (0.937)
  Pallas kernels: 92 us -> 86.1 us
    pallas_call x1, Pallas kernels: 92 us -> 86.1 us  [on_device(): pl.pallas_call(kernel, out_shape=jax.ShapeDtypeStruct((PIX, C), BF16), in...]
where the time goes in v3:
time: 88.9 us; the launch traced here: 88.8 us
  Pallas kernels  86.1 us (97%)
  local copies, waits for them, and re-layouts  2.73 us (3%)
    pallas_call x1, Pallas kernels, on_device(): pl.pallas_call(kernel, out_shape=jax.ShapeDtypeStruct((PIX, C), BF16), in...  86.1 us
    unnamed x1, local copies, waits for them, and re-layouts  2.73 us

profile of v3, /device:TPU:1, one launch (start us, length us, event | category | flops | bytes accessed | tf_op | source)
XLA Modules:
  0.0 88.8 jit_solution(12258965765212489762)
XLA Ops:
  0.0 86.1 %shard_map.100 = bf16[3072,256]{1,0:T(8,128)(2,1)} custom-call(bf16[3072,256]{1,0:T(8,128)(2,1)} %bitcast.7, f32[2,2,256]{2,1,0:T(2,128)} %gains_hbm.1, bf16[2,2304,256]{2,1,0:T(8,128)(2,1)} %bitcast.5, bf16[2,2304,256]{2,1,0:T(8,128)(2,1)} %bitcast.6, bf16[2,256,512]{2,1,0:T(8,128)(2,1)} %pin_hbm.1, bf16[2,256,256]{2,1,0:T(8,128)(2,1)} %bm_hbm.1, ...), custom_call_target="tpu_custom_call" | custom-call | tf_op jit(solution)/shard_map/pallas_call | solution.py:395
  86.1 2.7 %copy.12 = bf16[48,64,256]{2,1,0:T(8,128)(2,1)} copy(bf16[48,64,256]{2,1,0:T(8,128)(2,1)} %bitcast.4) | data formatting | bytes 3145728

commit v4 on v3

--- a/solution.py
+++ b/solution.py
@@ -83,9 +83,8 @@
     ]
     for copy in small:
         copy.start()
-    for l in range(LAYERS):
-        for i in range(len(weights)):
-            weight(i, l).start()
+    for i in range(len(weights)):
+        weight(i, 0).start()
 
     barrier = pltpu.get_barrier_semaphore()
 
@@ -115,7 +114,10 @@
         norm_rows(c, v, gains[0, 0:1, :])
         return carry
 
-    lax.fori_loop(0, CH // 4, first_norm, 0, unroll=2)
+    lax.fori_loop(0, CH // 4, first_norm, 0, unroll=3)
+    for l in range(1, LAYERS):
+        for i in range(len(weights)):
+            weight(i, l).start()
 
     def layer(l, carry):
         gain1 = gains[l, 1:2, :]
@@ -351,11 +353,11 @@
 
             @pl.when(l < LAYERS - 1)
             def _():
-                lax.fori_loop(6 * kappa, 6 * kappa + 6, middle, 0, unroll=2)
+                lax.fori_loop(6 * kappa, 6 * kappa + 6, middle, 0, unroll=3)
 
             @pl.when(l == LAYERS - 1)
             def _():
-                lax.fori_loop(6 * kappa, 6 * kappa + 6, last, 0, unroll=2)
+                lax.fori_loop(6 * kappa, 6 * kappa + 6, last, 0, unroll=3)
                 store(kappa).start()
 
         whole = GV.at[l, pl.ds(0, (CELLS - 1) * OCT)]

time: 88.9 us -> 88.2 us (level)
  no operation moved by 1% of the time
where the time goes in v4:
time: 88.2 us; the launch traced here: 88.1 us
  Pallas kernels  85.4 us (97%)
  local copies, waits for them, and re-layouts  2.73 us (3%)
    pallas_call x1, Pallas kernels, on_device(): pl.pallas_call(kernel, out_shape=jax.ShapeDtypeStruct((PIX, C), BF16), in...  85.4 us
    unnamed x1, local copies, waits for them, and re-layouts  2.73 us

profile of v4, /device:TPU:1, one launch (start us, length us, event | category | flops | bytes accessed | tf_op | source)
XLA Modules:
  0.0 88.1 jit_solution(3100950984454341311)
XLA Ops:
  0.0 85.4 %shard_map.100 = bf16[3072,256]{1,0:T(8,128)(2,1)} custom-call(bf16[3072,256]{1,0:T(8,128)(2,1)} %bitcast.7, f32[2,2,256]{2,1,0:T(2,128)} %gains_hbm.1, bf16[2,2304,256]{2,1,0:T(8,128)(2,1)} %bitcast.5, bf16[2,2304,256]{2,1,0:T(8,128)(2,1)} %bitcast.6, bf16[2,256,512]{2,1,0:T(8,128)(2,1)} %pin_hbm.1, bf16[2,256,256]{2,1,0:T(8,128)(2,1)} %bm_hbm.1, ...), custom_call_target="tpu_custom_call" | custom-call | tf_op jit(solution)/shard_map/pallas_call | solution.py:397
  85.4 2.7 %copy.12 = bf16[48,64,256]{2,1,0:T(8,128)(2,1)} copy(bf16[48,64,256]{2,1,0:T(8,128)(2,1)} %bitcast.4) | data formatting | bytes 3145728
